TPU v7x, 32 devices: a whole 2x2x4 slice. The times are simulated.
32 devices in a mesh: cell: 8 (over z, x), grp: 4 (over y, core).
Axes of the slice: x: 2, y: 2, z: 4, core: 2. Of those that a mesh axis runs over, the one named last changes fastest.
Arguments:
- atom_sites: float32 [3, 16384], P(None, ('cell', 'grp')), may hold values from 0 to 8, as said below
- grid_points: float32 [3, 12288], P(None, ('cell', 'grp')), may hold values from 0 to 8, as said below
- dipole_guess: float32 [3, 16384], P(None, ('cell', 'grp')), may hold values from -2 to 2
- fixed_field: float32 [3, 16384], P(None, ('cell', 'grp')), may hold values from -1800 to 1800
- polarisability: float32 [16384], P(('cell', 'grp')), may hold values from 0.0005 to 0.002
- base_charge: float32 [12288], P(('cell', 'grp')), may hold values from -12 to 12
- response: float32 [12288], P(('cell', 'grp')), may hold values from 0.02 to 0.2
- near_blocks: int32 [128, 8], P(('cell', 'grp')), may hold values from 0 to 47, as said below
- grid_blocks: int32 [128, 4], P(('cell', 'grp')), may hold values from 0 to 35, as said below
- source_blocks: int32 [96, 8], P(('cell', 'grp')), may hold values from 0 to 47, as said below
Outputs:
- dipoles: float32 [3, 16384], P(None, ('cell', 'grp'))
- qm_charges: float32 [12288], P(('cell', 'grp'))
Inputs may be any that keep to these rules, and one draw needn't show every extreme that they name: `atom_sites`: atom a has first coordinate in [c, c + 1) with c = a // 2048, the other two in [0, 1). `grid_points`: grid point g has first coordinate in [c, c + 1) with c = g // 1536, the other two in [0, 1). `near_blocks`: each row holds 8 distinct MM window indices, never the block's own index 16 + b % 16. `grid_blocks`: each row holds 4 distinct grid window indices. `source_blocks`: each row holds 8 distinct MM window indices.
All inputs are finite; a program needn't handle non-finite values.
Results may differ from a plain program's by a relative error of at most 0.0003.
Values sent between devices are 32-bit elements; how exact they have to be, the bound alone decides.
A program may use at most 64 MiB of HBM per device.

v0:
```python
import jax
import jax.numpy as jnp
from jax import lax
from jax.sharding import PartitionSpec as P

BLOCK = 128
ITERS = 3
soften_sq = 0.04


def with_halo(x, sides, width):
    for axis, dim in sides:
        peers, length = (lax.axis_size(axis), x.shape[dim])
        up = [(i, (i + 1) % peers) for i in range(peers - 1)]
        down = [(j, i) for i, j in up]
        last = lax.slice_in_dim(x, length - width, length, axis=dim)
        initial = lax.slice_in_dim(x, 0, width, axis=dim)
        before = lax.ppermute(last, axis, up)
        after = lax.ppermute(initial, axis, down)
        x = jnp.concatenate([before, x, after], axis=dim)
    return x


def pair_geometry(targets, sources):
    delta_x = targets[0][:, None] - sources[0][None, :]
    delta_y = targets[1][:, None] - sources[1][None, :]
    delta_z = targets[2][:, None] - sources[2][None, :]
    inverse = 1.0 / jnp.sqrt(delta_x * delta_x + delta_y * delta_y + delta_z * delta_z + soften_sq)
    inv_cube = inverse * inverse * inverse
    return (delta_x, delta_y, delta_z, inv_cube, inv_cube * inverse * inverse)


def dipole_field(targets, sources, moments, keep_mask):
    delta_x, delta_y, delta_z, inv_cube, inv_fifth = pair_geometry(targets, sources)
    projected = (
        moments[0][None, :] * delta_x
        + moments[1][None, :] * delta_y
        + moments[2][None, :] * delta_z
    )
    radial = 3.0 * projected * inv_fifth * keep_mask
    direct = inv_cube * keep_mask
    return jnp.stack(
        [
            jnp.sum(radial * delta_x - moments[0][None, :] * direct, axis=1),
            jnp.sum(radial * delta_y - moments[1][None, :] * direct, axis=1),
            jnp.sum(radial * delta_z - moments[2][None, :] * direct, axis=1),
        ]
    )


def charge_field(targets, sources, charges):
    delta_x, delta_y, delta_z, inv_cube, inv_fifth = pair_geometry(targets, sources)
    weight = charges[None, :] * inv_cube
    return jnp.stack(
        [
            jnp.sum(weight * delta_x, axis=1),
            jnp.sum(weight * delta_y, axis=1),
            jnp.sum(weight * delta_z, axis=1),
        ]
    )


def dipole_potential(targets, sources, moments):
    delta_x, delta_y, delta_z, inv_cube, inv_fifth = pair_geometry(targets, sources)
    projected = (
        moments[0][None, :] * delta_x
        + moments[1][None, :] * delta_y
        + moments[2][None, :] * delta_z
    )
    return jnp.sum(projected * inv_cube, axis=1)


def far_geometry(targets, cell_here, cell_count):
    centres = jnp.arange(cell_count, dtype=jnp.int32).astype(jnp.float32) + 0.5
    delta_x = targets[0][None, :] - centres[:, None]
    delta_y = targets[1][None, :] - 0.5
    delta_z = targets[2][None, :] - 0.5
    far_mask = (jnp.abs(jnp.arange(cell_count, dtype=jnp.int32) - cell_here) >= 2).astype(
        jnp.float32
    )[:, None]
    inverse = 1.0 / jnp.sqrt(delta_x * delta_x + delta_y * delta_y + delta_z * delta_z + soften_sq)
    inv_cube = inverse * inverse * inverse * far_mask
    return (delta_x, delta_y, delta_z, inv_cube, inv_cube * inverse * inverse)


def far_field(targets, cell_here, moments, charges):
    delta_x, delta_y, delta_z, inv_cube, inv_fifth = far_geometry(
        targets, cell_here, charges.shape[0]
    )
    projected = moments[:, 0:1] * delta_x + moments[:, 1:2] * delta_y + moments[:, 2:3] * delta_z
    radial = 3.0 * projected * inv_fifth
    coulomb = charges[:, None] * inv_cube
    return jnp.stack(
        [
            jnp.sum(radial * delta_x - moments[:, 0:1] * inv_cube + coulomb * delta_x, axis=0),
            jnp.sum(radial * delta_y - moments[:, 1:2] * inv_cube + coulomb * delta_y, axis=0),
            jnp.sum(radial * delta_z - moments[:, 2:3] * inv_cube + coulomb * delta_z, axis=0),
        ]
    )


def far_potential(targets, cell_here, moments):
    delta_x, delta_y, delta_z, inv_cube, inv_fifth = far_geometry(
        targets, cell_here, moments.shape[0]
    )
    projected = moments[:, 0:1] * delta_x + moments[:, 1:2] * delta_y + moments[:, 2:3] * delta_z
    return jnp.sum(projected * inv_cube, axis=0)


def listed_tiles(tile_set, index_lists):
    taken = jnp.take(tile_set, index_lists, axis=1)
    count, listed = index_lists.shape
    return jnp.transpose(taken, (1, 0, 2, 3)).reshape(count, 3, listed * tile_set.shape[2])


def spread(payload):
    lifted = payload[:, None, None, :]
    with_rims = with_halo(lifted, (("cell", 1),), 1)
    return lax.all_gather(with_rims, "grp", axis=2, tiled=True)


def body(
    atom_sites,
    grid_points,
    dipole_guess,
    fixed_field,
    polarisability,
    base_charge,
    response,
    near_blocks,
    grid_blocks,
    source_blocks,
):
    groups = lax.axis_size("grp")
    cell_here = lax.axis_index("cell")
    grp_here = lax.axis_index("grp")
    local_blocks = near_blocks.shape[0]
    local_gblocks = source_blocks.shape[0]
    atom_count = atom_sites.shape[1]
    grid_count = grid_points.shape[1]
    cell_blocks = local_blocks * groups
    cell_gblocks = local_gblocks * groups
    statics = spread(jnp.concatenate([atom_sites, grid_points], axis=1))
    site_tiles = statics[:, :, :, :atom_count].reshape(3, 3 * cell_blocks, BLOCK)
    point_tiles = statics[:, :, :, atom_count:].reshape(3, 3 * cell_gblocks, BLOCK)
    atom_targets = jnp.transpose(atom_sites.reshape(3, local_blocks, BLOCK), (1, 0, 2))
    grid_targets = jnp.transpose(grid_points.reshape(3, local_gblocks, BLOCK), (1, 0, 2))
    own_slots = cell_blocks + grp_here * local_blocks + jnp.arange(local_blocks, dtype=jnp.int32)
    atom_lists = jnp.concatenate([own_slots[:, None], near_blocks], axis=1)
    near_sites = listed_tiles(site_tiles, atom_lists)
    grid_sites = listed_tiles(point_tiles, grid_blocks)
    source_sites = listed_tiles(site_tiles, source_blocks)
    keep_mask = jnp.concatenate(
        [
            1.0 - jnp.eye(BLOCK, dtype=jnp.float32),
            jnp.ones((BLOCK, near_blocks.shape[1] * BLOCK), jnp.float32),
        ],
        axis=1,
    )
    centre = jnp.stack(
        [
            cell_here.astype(jnp.float32) + 0.5,
            jnp.array(0.5, jnp.float32),
            jnp.array(0.5, jnp.float32),
        ]
    )
    offsets = grid_points - centre[:, None]
    dipoles = dipole_guess
    charges = base_charge
    for iteration in range(ITERS):
        shared = spread(jnp.concatenate([dipoles, charges.reshape(3, grid_count // 3)], axis=1))
        dipole_tiles = shared[:, :, :, :atom_count].reshape(3, 3 * cell_blocks, BLOCK)
        charge_tiles = jnp.transpose(shared[:, :, :, atom_count:], (1, 2, 0, 3)).reshape(
            3 * cell_gblocks, BLOCK
        )
        local_sums = jnp.concatenate(
            [
                jnp.sum(dipoles, axis=1),
                jnp.sum(charges)[None],
                jnp.sum(charges[None, :] * offsets, axis=1),
            ]
        )
        cell_sums = lax.psum(local_sums, "grp")
        moment_table = lax.all_gather(cell_sums[None, :], "cell", axis=0, tiled=True)
        dipole_sums = moment_table[:, 0:3]
        charge_sums = moment_table[:, 3]
        moments = dipole_sums + moment_table[:, 4:7]
        near_dipoles = listed_tiles(dipole_tiles, atom_lists)
        source_dipoles = listed_tiles(dipole_tiles, source_blocks)
        grid_charges = jnp.take(charge_tiles, grid_blocks, axis=0).reshape(local_blocks, -1)

        def one_atom_block(block_args):
            targets, sources, source_moments, points, point_charges = block_args
            accumulated = dipole_field(targets, sources, source_moments, keep_mask)
            accumulated = accumulated + charge_field(targets, points, point_charges)
            return accumulated + far_field(targets, cell_here, moments, charge_sums)

        def one_grid_block(block_args):
            targets, sources, source_moments = block_args
            return dipole_potential(targets, sources, source_moments) + far_potential(
                targets, cell_here, dipole_sums
            )

        induced_field = lax.map(
            one_atom_block, (atom_targets, near_sites, near_dipoles, grid_sites, grid_charges)
        )
        induced_field = jnp.transpose(induced_field, (1, 0, 2)).reshape(3, atom_count)
        potential = lax.map(one_grid_block, (grid_targets, source_sites, source_dipoles)).reshape(
            grid_count
        )
        dipoles = polarisability[None, :] * (fixed_field + induced_field)
        charges = base_charge - response * potential
    return (dipoles, charges)


def solution(mesh):
    return jax.shard_map(
        body,
        mesh=mesh,
        in_specs=(
            P(None, ("cell", "grp")),
            P(None, ("cell", "grp")),
            P(None, ("cell", "grp")),
            P(None, ("cell", "grp")),
            P(("cell", "grp")),
            P(("cell", "grp")),
            P(("cell", "grp")),
            P(("cell", "grp"), None),
            P(("cell", "grp"), None),
            P(("cell", "grp"), None),
        ),
        out_specs=(P(None, ("cell", "grp")), P(("cell", "grp"))),
        check_vma=False,
    )
```

profile of v0, /device:TPU:0, one launch (start us, length us, event | category | flops | bytes accessed | tf_op | source)
XLA Modules:
  0.0 166.5 jit_solution(10735519480641597523)
XLA Ops:
  0.6 0.7 maximum_bitcast_fusion.1
  1.4 1.3 collective-permute-start.1
  2.7 5.5 %collective-permute-start = (f32[3,1,1,640]{3,0,2,1:T(4,128)S(1)}, f32[3,1,1,640]{3,0,2,1:T(4,128)S(1)}, u32[]{:S(2)}, u32[]{:S(2)}) collective-permute-start(f32[3,1,1,640]{3,0,2,1:T(4,128)S(1)} %maximum_bitcast_fusion.1), channel_id=1, source_target_pairs={{0,4},{4,8},{8,12},{12,16},{16,20},{20,24},{24,28},{1,5},{5,9},{9,... | collective-permute-start | bytes 23048 | tf_op jit(solution)/shard_map/ppermute | solution.py:18
  8.2 1.3 collective-permute-start.3
  9.5 5.4 %collective-permute-start.2 = (f32[3,1,1,896]{3,0,2,1:T(4,128)S(1)}, f32[3,1,1,896]{3,0,2,1:T(4,128)S(1)}, u32[]{:S(2)}, u32[]{:S(2)}) collective-permute-start(f32[3,1,1,896]{3,0,2,1:T(4,128)S(1)} %maximum_bitcast_fusion), channel_id=1, source_target_pairs={{0,4},{4,8},{8,12},{12,16},{16,20},{20,24},{24,28},{1,5},{5,9},{9,... | collective-permute-start | bytes 32264 | tf_op jit(solution)/shard_map/ppermute | solution.py:18
  15.0 0.7 copy-done.8
  15.8 0.7 copy-done.2
  17.3 0.7 maximum_bitcast_fusion.4
  18.0 5.7 %psum.21 = f32[1,7]{1,0:T(1,128)S(1)} all-reduce(f32[1,7]{1,0:T(1,128)S(1)} %maximum_bitcast_fusion.4), channel_id=1, replica_groups=mesh['cell'=8,'grp'=4] {'grp'}, use_global_device_ids=true, to_apply=%region_3.6 | all-reduce | flops 7 | bytes 56 | tf_op jit(solution)/shard_map/psum | solution.py:183
  23.8 0.7 copy-done.9
  24.8 19.3 %all-gather = f32[8,1,7]{2,1,0:T(1,128)S(1)} all-gather(f32[1,1,7]{2,1,0:T(1,128)S(1)} %bitcast.636), channel_id=1, replica_groups=mesh['cell'=8,'grp'=4] {'cell'}, dimensions={0}, use_global_device_ids=true | all-gather | bytes 252 | tf_op jit(solution)/shard_map/all_gather | solution.py:184
  44.6 5.4 %all_gather.21 = f32[3,3,4,640]{3,0,2,1:T(4,128)S(1)} all-gather(f32[3,3,1,640]{3,0,2,1:T(4,128)S(1)} %pad_maximum_fusion.1), channel_id=1, replica_groups=mesh['cell'=8,'grp'=4] {'grp'}, dimensions={2}, use_global_device_ids=true | all-gather | bytes 115200 | tf_op jit(solution)/shard_map/all_gather | solution.py:119
  51.3 0.6 gather_fusion.1
  51.9 5.6 %all_gather.22 = f32[3,3,4,896]{3,0,2,1:T(4,128)S(1)} all-gather(f32[3,3,1,896]{3,0,2,1:T(4,128)S(1)} %pad_maximum_fusion), channel_id=1, replica_groups=mesh['cell'=8,'grp'=4] {'grp'}, dimensions={2}, use_global_device_ids=true | all-gather | bytes 161280 | tf_op jit(solution)/shard_map/all_gather | solution.py:119
  58.1 0.6 gather_fusion.2
  59.7 2.4 %while.79 = (s32[]{:T(128)}, f32[3,128]{1,0:T(4,128)S(1)}, f32[3,3,1024]{2,0,1:T(4,128)S(1)}, f32[3,3,128]{2,1,0:T(4,128)S(1)}, f32[3,3,1024]{2,1,0:T(4,128)S(1)...) while((s32[]{:T(128)}, f32[3,128]{1,0:T(4,128)S(1)}, ...), condition=%wide.region_18.22_spmd, body=%wide.region_15.21_spmd.sunk | while | flops 2375092 | bytes 91217 | solution.py:208
  62.1 0.6 fusion.190
  63.1 6.3 %while.78 = (s32[]{:T(128)}, f32[4,3,128]{2,1,0:T(4,128)S(1)}, f32[4,3,1152]{2,1,0:T(4,128)S(1)}, f32[4,3,128]{2,1,0:T(4,128)S(1)}, f32[4,3,1152]{2,1,0:T(4,128)...) while((s32[]{:T(128)}, f32[4,3,128]{2,1,0:T(4,128)S(1)}, ...), condition=%wide.region_14.17_spmd, body=%wide.region_4.16_spmd.sunk | while | flops 6232500 | bytes 724117 | solution.py:204
  63.7 0.9 fusion.208
  65.3 0.9 fusion.208
  66.9 0.9 fusion.208
  68.5 0.9 fusion.208
  69.6 1.3 collective-permute-start.5
  70.9 0.7 maximum_bitcast_fusion.5
  71.5 4.5 %collective-permute-start.4 = (f32[3,1,1,640]{3,0,2,1:T(4,128)S(1)}, f32[3,1,1,640]{3,0,2,1:T(4,128)S(1)}, u32[]{:S(2)}, u32[]{:S(2)}) collective-permute-start(f32[3,1,1,640]{3,0,2,1:T(4,128)S(1)} %maximum_bitcast_fusion.2), channel_id=1, source_target_pairs={{0,4},{4,8},{8,12},{12,16},{16,20},{20,24},{24,28},{1,5},{5,9},{9,... | collective-permute-start | bytes 23048 | tf_op jit(solution)/shard_map/ppermute | solution.py:18
  76.1 7.0 %psum.22 = f32[1,7]{1,0:T(1,128)S(1)} all-reduce(f32[1,7]{1,0:T(1,128)S(1)} %maximum_bitcast_fusion.5), channel_id=1, replica_groups=mesh['cell'=8,'grp'=4] {'grp'}, use_global_device_ids=true, to_apply=%region_22.26 | all-reduce | flops 7 | bytes 56 | tf_op jit(solution)/shard_map/psum | solution.py:183
  83.1 16.3 %all-gather.1 = f32[8,1,7]{2,1,0:T(1,128)S(1)} all-gather(f32[1,1,7]{2,1,0:T(1,128)S(1)} %bitcast.637), channel_id=1, replica_groups=mesh['cell'=8,'grp'=4] {'cell'}, dimensions={0}, use_global_device_ids=true | all-gather | bytes 252 | tf_op jit(solution)/shard_map/all_gather | solution.py:184
  99.8 5.4 %all_gather.24 = f32[3,3,4,640]{3,0,2,1:T(4,128)S(1)} all-gather(f32[3,3,1,640]{3,0,2,1:T(4,128)S(1)} %pad_maximum_fusion.2), channel_id=1, replica_groups=mesh['cell'=8,'grp'=4] {'grp'}, dimensions={2}, use_global_device_ids=true | all-gather | bytes 115200 | tf_op jit(solution)/shard_map/all_gather | solution.py:119
  105.9 0.6 gather_fusion.6
  107.3 6.3 %while.80 = (s32[]{:T(128)}, f32[4,3,128]{2,1,0:T(4,128)S(1)}, f32[4,3,1152]{2,1,0:T(4,128)S(1)}, f32[4,3,128]{2,1,0:T(4,128)S(1)}, f32[4,3,1152]{2,1,0:T(4,128)...) while((s32[]{:T(128)}, f32[4,3,128]{2,1,0:T(4,128)S(1)}, ...), condition=%wide.region_33.37_spmd, body=%wide.region_23.36_spmd.sunk | while | flops 6232500 | bytes 724117 | solution.py:204
  108.0 0.9 fusion.213
  109.6 0.9 fusion.213
  111.2 0.9 fusion.213
  112.8 0.9 fusion.213
  113.8 2.4 %while.81 = (s32[]{:T(128)}, f32[3,128]{1,0:T(4,128)S(1)}, f32[3,3,1024]{2,0,1:T(4,128)S(1)}, f32[3,3,128]{2,1,0:T(4,128)S(1)}, f32[3,3,1024]{2,1,0:T(4,128)S(1)...) while((s32[]{:T(128)}, f32[3,128]{1,0:T(4,128)S(1)}, ...), condition=%wide.region_37.41_spmd, body=%wide.region_34.40_spmd.sunk | while | flops 2375092 | bytes 91217 | solution.py:208
  117.1 1.3 collective-permute-start.7
  118.4 0.7 maximum_bitcast_fusion.6
  119.1 4.5 %collective-permute-start.6 = (f32[3,1,1,640]{3,0,2,1:T(4,128)S(1)}, f32[3,1,1,640]{3,0,2,1:T(4,128)S(1)}, u32[]{:S(2)}, u32[]{:S(2)}) collective-permute-start(f32[3,1,1,640]{3,0,2,1:T(4,128)S(1)} %maximum_bitcast_fusion.3), channel_id=1, source_target_pairs={{0,4},{4,8},{8,12},{12,16},{16,20},{20,24},{24,28},{1,5},{5,9},{9,... | collective-permute-start | bytes 23048 | tf_op jit(solution)/shard_map/ppermute | solution.py:18
  123.6 5.8 %psum.23 = f32[1,7]{1,0:T(1,128)S(1)} all-reduce(f32[1,7]{1,0:T(1,128)S(1)} %maximum_bitcast_fusion.6), channel_id=1, replica_groups=mesh['cell'=8,'grp'=4] {'grp'}, use_global_device_ids=true, to_apply=%region_41.45 | all-reduce | flops 7 | bytes 56 | tf_op jit(solution)/shard_map/psum | solution.py:183
  129.4 19.2 %all-gather.2 = f32[8,1,7]{2,1,0:T(1,128)S(1)} all-gather(f32[1,1,7]{2,1,0:T(1,128)S(1)} %bitcast.638), channel_id=1, replica_groups=mesh['cell'=8,'grp'=4] {'cell'}, dimensions={0}, use_global_device_ids=true | all-gather | bytes 252 | tf_op jit(solution)/shard_map/all_gather | solution.py:184
  149.0 5.4 %all_gather.26 = f32[3,3,4,640]{3,0,2,1:T(4,128)S(1)} all-gather(f32[3,3,1,640]{3,0,2,1:T(4,128)S(1)} %pad_maximum_fusion.3), channel_id=1, replica_groups=mesh['cell'=8,'grp'=4] {'grp'}, dimensions={2}, use_global_device_ids=true | all-gather | bytes 115200 | tf_op jit(solution)/shard_map/all_gather | solution.py:119
  155.0 0.6 gather_fusion.9
  156.5 6.3 %while.82 = (s32[]{:T(128)}, f32[4,3,128]{2,1,0:T(4,128)S(1)}, f32[4,3,1152]{2,1,0:T(4,128)S(1)}, f32[4,3,128]{2,1,0:T(4,128)S(1)}, f32[4,3,1152]{2,1,0:T(4,128)...) while((s32[]{:T(128)}, f32[4,3,128]{2,1,0:T(4,128)S(1)}, ...), condition=%wide.region_52.56_spmd, body=%wide.region_42.55_spmd.sunk | while | flops 6232500 | bytes 724117 | solution.py:204
  157.2 0.9 fusion.218
  158.7 0.9 fusion.218
  160.3 0.9 fusion.218
  161.9 0.9 fusion.218
  163.5 2.4 %while.83 = (s32[]{:T(128)}, f32[3,128]{1,0:T(4,128)S(1)}, f32[3,3,1024]{2,0,1:T(4,128)S(1)}, f32[3,3,128]{2,1,0:T(4,128)S(1)}, f32[3,3,1024]{2,1,0:T(4,128)S(1)...) while((s32[]{:T(128)}, f32[3,128]{1,0:T(4,128)S(1)}, ...), condition=%wide.region_56.60_spmd, body=%wide.region_53.59_spmd.sunk | while | flops 2375092 | bytes 91217 | solution.py:208
  (370 shorter events, 24.8 us)
Async XLA Ops:
  0.6 7.5 %copy-start = (f32[3,384]{1,0:T(4,128)S(1)}, f32[3,384]{1,0:T(4,128)}, u32[]{:S(2)}) copy-start(f32[3,384]{1,0:T(4,128)} %param.29) | copy-start | bytes 13828
  0.6 7.5 %copy-start.1 = (f32[3,512]{1,0:T(4,128)S(1)}, f32[3,512]{1,0:T(4,128)}, u32[]{:S(2)}) copy-start(f32[3,512]{1,0:T(4,128)} %param.28) | copy-start | bytes 18436
  1.4 43.2 %collective-permute-start.1 = (f32[3,1,1,640]{3,0,2,1:T(4,128)S(1)}, f32[3,1,1,640]{3,0,2,1:T(4,128)S(1)}, u32[]{:S(2)}, u32[]{:S(2)}) collective-permute-start(f32[3,1,1,640]{3,0,2,1:T(4,128)S(1)} %maximum_bitcast_fusion.1), channel_id=1, source_target_pairs={{4,0},{8,4},{12,8},{16,12},{20,16},{24,20},{28,24},{5,1},{9,5},{13... | collective-permute-start | bytes 23048 | tf_op jit(solution)/shard_map/ppermute | solution.py:19
  2.7 41.9 %collective-permute-start = (f32[3,1,1,640]{3,0,2,1:T(4,128)S(1)}, f32[3,1,1,640]{3,0,2,1:T(4,128)S(1)}, u32[]{:S(2)}, u32[]{:S(2)}) collective-permute-start(f32[3,1,1,640]{3,0,2,1:T(4,128)S(1)} %maximum_bitcast_fusion.1), channel_id=1, source_target_pairs={{0,4},{4,8},{8,12},{12,16},{16,20},{20,24},{24,28},{1,5},{5,9},{9,... | collective-permute-start | bytes 23048 | tf_op jit(solution)/shard_map/ppermute | solution.py:18
  8.2 6.8 %copy-start.7 = (s32[4,4]{1,0:T(4,128)S(1)}, s32[4,4]{1,0:T(4,128)}, u32[]{:S(2)}) copy-start(s32[4,4]{1,0:T(4,128)} %param.36) | copy-start | bytes 196
  8.2 43.7 %collective-permute-start.3 = (f32[3,1,1,896]{3,0,2,1:T(4,128)S(1)}, f32[3,1,1,896]{3,0,2,1:T(4,128)S(1)}, u32[]{:S(2)}, u32[]{:S(2)}) collective-permute-start(f32[3,1,1,896]{3,0,2,1:T(4,128)S(1)} %maximum_bitcast_fusion), channel_id=1, source_target_pairs={{4,0},{8,4},{12,8},{16,12},{20,16},{24,20},{28,24},{5,1},{9,5},{13... | collective-permute-start | bytes 32264 | tf_op jit(solution)/shard_map/ppermute | solution.py:19
  9.5 42.4 %collective-permute-start.2 = (f32[3,1,1,896]{3,0,2,1:T(4,128)S(1)}, f32[3,1,1,896]{3,0,2,1:T(4,128)S(1)}, u32[]{:S(2)}, u32[]{:S(2)}) collective-permute-start(f32[3,1,1,896]{3,0,2,1:T(4,128)S(1)} %maximum_bitcast_fusion), channel_id=1, source_target_pairs={{0,4},{4,8},{8,12},{12,16},{16,20},{20,24},{24,28},{1,5},{5,9},{9,... | collective-permute-start | bytes 32264 | tf_op jit(solution)/shard_map/ppermute | solution.py:18
  15.0 0.7 copy-start.8
  15.7 0.7 copy-start.2
  15.7 1.3 copy-start.4
  23.8 0.7 copy-start.9
  59.6 2.4 %copy-start.5 = (f32[384]{0:T(512)S(1)}, f32[384]{0:T(512)}, u32[]{:S(2)}) copy-start(f32[384]{0:T(512)} %param.34) | copy-start | bytes 4612
  63.0 6.4 %copy-start.3 = (f32[3,512]{1,0:T(4,128)S(1)}, f32[3,512]{1,0:T(4,128)}, u32[]{:S(2)}) copy-start(f32[3,512]{1,0:T(4,128)} %param.31) | copy-start | bytes 18436
  63.0 6.4 %copy-start.6 = (f32[512]{0:T(512)S(1)}, f32[512]{0:T(512)}, u32[]{:S(2)}) copy-start(f32[512]{0:T(512)} %param.32) | copy-start | bytes 6148
  69.6 30.3 %collective-permute-start.5 = (f32[3,1,1,640]{3,0,2,1:T(4,128)S(1)}, f32[3,1,1,640]{3,0,2,1:T(4,128)S(1)}, u32[]{:S(2)}, u32[]{:S(2)}) collective-permute-start(f32[3,1,1,640]{3,0,2,1:T(4,128)S(1)} %maximum_bitcast_fusion.2), channel_id=1, source_target_pairs={{4,0},{8,4},{12,8},{16,12},{20,16},{24,20},{28,24},{5,1},{9,5},{13... | collective-permute-start | bytes 23048 | tf_op jit(solution)/shard_map/ppermute | solution.py:19
  71.5 28.3 %collective-permute-start.4 = (f32[3,1,1,640]{3,0,2,1:T(4,128)S(1)}, f32[3,1,1,640]{3,0,2,1:T(4,128)S(1)}, u32[]{:S(2)}, u32[]{:S(2)}) collective-permute-start(f32[3,1,1,640]{3,0,2,1:T(4,128)S(1)} %maximum_bitcast_fusion.2), channel_id=1, source_target_pairs={{0,4},{4,8},{8,12},{12,16},{16,20},{20,24},{24,28},{1,5},{5,9},{9,... | collective-permute-start | bytes 23048 | tf_op jit(solution)/shard_map/ppermute | solution.py:18
  117.1 31.9 %collective-permute-start.7 = (f32[3,1,1,640]{3,0,2,1:T(4,128)S(1)}, f32[3,1,1,640]{3,0,2,1:T(4,128)S(1)}, u32[]{:S(2)}, u32[]{:S(2)}) collective-permute-start(f32[3,1,1,640]{3,0,2,1:T(4,128)S(1)} %maximum_bitcast_fusion.3), channel_id=1, source_target_pairs={{4,0},{8,4},{12,8},{16,12},{20,16},{24,20},{28,24},{5,1},{9,5},{13... | collective-permute-start | bytes 23048 | tf_op jit(solution)/shard_map/ppermute | solution.py:19
  119.1 29.9 %collective-permute-start.6 = (f32[3,1,1,640]{3,0,2,1:T(4,128)S(1)}, f32[3,1,1,640]{3,0,2,1:T(4,128)S(1)}, u32[]{:S(2)}, u32[]{:S(2)}) collective-permute-start(f32[3,1,1,640]{3,0,2,1:T(4,128)S(1)} %maximum_bitcast_fusion.3), channel_id=1, source_target_pairs={{0,4},{4,8},{8,12},{12,16},{16,20},{20,24},{24,28},{1,5},{5,9},{9,... | collective-permute-start | bytes 23048 | tf_op jit(solution)/shard_map/ppermute | solution.py:18
where the time goes:
time: 167 us; the launch traced here: 166 us
  blocking collectives  95.1 us (57%)
  other arithmetic  30.4 us (18%)
  starting transfers between devices  25.2 us (15%)
  local copies, waits for them, and re-layouts  13.1 us (8%)
    all_gather x3, blocking collectives, body(): lax.all_gather(cell_sums[None, :], 'cell', axis=0, tiled=True)  54.8 us
    all_gather x4, blocking collectives, spread(): return lax.all_gather(with_rims, 'grp', axis=2, tiled=True)  21.7 us
    ppermute x4, starting transfers between devices, with_halo(): before = lax.ppermute(last, axis, up)  20 us
    psum x3, blocking collectives, body(): cell_sums = lax.psum(local_sums, 'grp')  18.6 us
    reduce_sum x12, other arithmetic, dipole_field(): jnp.sum(radial * delta_x - moments[0][None, :] * direct, axis=1)  10.7 us
    gather x10, local copies, waits for them, and re-layouts, listed_tiles(): taken = jnp.take(tile_set, index_lists, axis=1)  5.42 us
    ppermute x4, starting transfers between devices, with_halo(): after = lax.ppermute(initial, axis, down)  5.16 us
    reduce_sum x9, other arithmetic, dipole_potential(): return jnp.sum(projected * inv_cube, axis=1)  4.71 us
  transfers between devices with their start and end apart: 8, of which 0 were waited for; matrix products, arithmetic and copies ran while one was open for 4% of the time, Pallas kernels for 0%

commit v1 on v0

--- a/solution.py
+++ b/solution.py
@@ -180,7 +180,11 @@
                 jnp.sum(charges[None, :] * offsets, axis=1),
             ]
         )
-        cell_sums = lax.psum(local_sums, "grp")
+        cell_sums = local_sums
+        for hop in (1, 2):
+            cell_sums = cell_sums + lax.ppermute(
+                cell_sums, "grp", [(dev, dev ^ hop) for dev in range(4)]
+            )
         moment_table = lax.all_gather(cell_sums[None, :], "cell", axis=0, tiled=True)
         dipole_sums = moment_table[:, 0:3]
         charge_sums = moment_table[:, 3]

time: 167 us -> 169 us (1.012)
  blocking collectives: 95.1 us -> 79.1 us
  waiting for transfers between devices: 0.02 us -> 8.42 us
  starting transfers between devices: 25.2 us -> 29.9 us
  other arithmetic: 30.4 us -> 32.7 us
  local copies, waits for them, and re-layouts: 13.1 us -> 15.2 us
    unnamed x0 -> x3, blocking collectives: none -> 57.4 us
    all_gather x3 -> x0, blocking collectives: 54.8 us -> none  [body(): lax.all_gather(cell_sums[None, :], 'cell', axis=0, tiled=True)]
    psum x3 -> x0, blocking collectives: 18.6 us -> none  [body(): cell_sums = lax.psum(local_sums, 'grp')]
    ppermute x0 -> x6, waiting for transfers between devices: none -> 8.4 us  [body(): lax.ppermute(cell_sums, 'grp', [(dev, dev ^ hop) for dev in range(4)])]
    ppermute x0 -> x6, starting transfers between devices: none -> 4.66 us  [body(): lax.ppermute(cell_sums, 'grp', [(dev, dev ^ hop) for dev in range(4)])]
    broadcast_in_dim x3 -> x0, other arithmetic: 2.13 us -> none  [body(): cell_sums[None, :]]
    concatenate x0 -> x3, other arithmetic: none -> 2.09 us  [body(): jnp.concatenate([jnp.sum(dipoles, axis=1), jnp.sum(charges)[None], jnp.su...]
    add x0 -> x3, other arithmetic: none -> 2.09 us  [body(): cell_sums + lax.ppermute(cell_sums, 'grp', [(dev, dev ^ hop) for dev in r...]
  transfers between devices with their start and end apart: 8 -> 14, of which waited for: 0 -> 5; matrix products, arithmetic and copies ran while one was open for 4% -> 6% of each run, Pallas kernels for 0% -> 0%
where the time goes in v1:
time: 169 us
  blocking collectives  79.1 us (47%)
  other arithmetic  32.7 us (19%)
  starting transfers between devices  29.9 us (18%)
  local copies, waits for them, and re-layouts  15.2 us (9%)
  waiting for transfers between devices  8.42 us (5%)
  between operations  1.75 us (1%)
    unnamed x3, blocking collectives  57.4 us
    all_gather x4, blocking collectives, spread(): return lax.all_gather(with_rims, 'grp', axis=2, tiled=True)  21.7 us
    ppermute x4, starting transfers between devices, with_halo(): before = lax.ppermute(last, axis, up)  20 us
    reduce_sum x12, other arithmetic, dipole_field(): jnp.sum(radial * delta_x - moments[0][None, :] * direct, axis=1)  10.7 us
    ppermute x6, waiting for transfers between devices, body(): lax.ppermute(cell_sums, 'grp', [(dev, dev ^ hop) for dev in range(4)])  8.4 us
    gather x10, local copies, waits for them, and re-layouts, listed_tiles(): taken = jnp.take(tile_set, index_lists, axis=1)  5.42 us
    ppermute x4, starting transfers between devices, with_halo(): after = lax.ppermute(initial, axis, down)  5.16 us
    reduce_sum x9, other arithmetic, dipole_potential(): return jnp.sum(projected * inv_cube, axis=1)  4.71 us
  transfers between devices with their start and end apart: 14, of which 5 were waited for; matrix products, arithmetic and copies ran while one was open for 6% of the time, Pallas kernels for 0%

profile of v1, /device:TPU:0, one launch (start us, length us, event | category | flops | bytes accessed | tf_op | source)
XLA Modules:
  0.0 168.7 jit_solution(6692084338087165066)
XLA Ops:
  0.6 0.7 maximum_bitcast_fusion.1
  1.4 1.3 collective-permute-start.1
  2.7 5.5 %collective-permute-start = (f32[3,1,1,640]{3,0,2,1:T(4,128)S(1)}, f32[3,1,1,640]{3,0,2,1:T(4,128)S(1)}, u32[]{:S(2)}, u32[]{:S(2)}) collective-permute-start(f32[3,1,1,640]{3,0,2,1:T(4,128)S(1)} %maximum_bitcast_fusion.1), channel_id=1, source_target_pairs={{0,4},{4,8},{8,12},{12,16},{16,20},{20,24},{24,28},{1,5},{5,9},{9,... | collective-permute-start | bytes 23048 | tf_op jit(solution)/shard_map/ppermute | solution.py:18
  8.2 1.3 collective-permute-start.3
  9.5 5.4 %collective-permute-start.2 = (f32[3,1,1,896]{3,0,2,1:T(4,128)S(1)}, f32[3,1,1,896]{3,0,2,1:T(4,128)S(1)}, u32[]{:S(2)}, u32[]{:S(2)}) collective-permute-start(f32[3,1,1,896]{3,0,2,1:T(4,128)S(1)} %maximum_bitcast_fusion), channel_id=1, source_target_pairs={{0,4},{4,8},{8,12},{12,16},{16,20},{20,24},{24,28},{1,5},{5,9},{9,... | collective-permute-start | bytes 32264 | tf_op jit(solution)/shard_map/ppermute | solution.py:18
  16.6 0.7 pad_maximum_fusion.4
  21.6 0.7 fusion.195
  22.3 1.5 collective-permute-start.5
  23.8 2.0 %collective-permute-done.5 = f32[7]{0:T(128)S(1)} collective-permute-done((f32[7]{0:T(128)S(1)}, f32[7]{0:T(128)S(1)}, u32[]{:S(2)}, u32[]{:S(2)}) %collective-permute-start.5) | collective-permute-done | bytes 60 | tf_op jit(solution)/shard_map/ppermute | solution.py:185
  26.0 20.3 %all-reduce.2 = f32[56]{0:T(128)S(1)} all-reduce(f32[56]{0:T(128)S(1)} %add_dynamic-update-slice_fusion.2), channel_id=2, replica_groups=mesh['cell'=8,'grp'=4] {'cell'}, use_global_device_ids=true, to_apply=%add.2 | all-reduce | flops 56 | bytes 448
  46.7 5.4 %all_gather.21 = f32[3,3,4,640]{3,0,2,1:T(4,128)S(1)} all-gather(f32[3,3,1,640]{3,0,2,1:T(4,128)S(1)} %pad_maximum_fusion.1), channel_id=1, replica_groups=mesh['cell'=8,'grp'=4] {'grp'}, dimensions={2}, use_global_device_ids=true | all-gather | bytes 115200 | tf_op jit(solution)/shard_map/all_gather | solution.py:119
  54.1 5.5 %all_gather.22 = f32[3,3,4,896]{3,0,2,1:T(4,128)S(1)} all-gather(f32[3,3,1,896]{3,0,2,1:T(4,128)S(1)} %pad_maximum_fusion), channel_id=1, replica_groups=mesh['cell'=8,'grp'=4] {'grp'}, dimensions={2}, use_global_device_ids=true | all-gather | bytes 161280 | tf_op jit(solution)/shard_map/all_gather | solution.py:119
  61.8 2.4 %while.79 = (s32[]{:T(128)}, f32[3,128]{1,0:T(4,128)S(1)}, f32[3,3,1024]{2,0,1:T(4,128)S(1)}, f32[3,3,128]{2,1,0:T(4,128)S(1)}, f32[3,3,1024]{2,1,0:T(4,128)S(1)...) while((s32[]{:T(128)}, f32[3,128]{1,0:T(4,128)S(1)}, ...), condition=%wide.region_17.21_spmd, body=%wide.region_14.20_spmd.sunk | while | flops 2375092 | bytes 91217 | solution.py:212
  65.2 6.3 %while.78 = (s32[]{:T(128)}, f32[4,3,128]{2,1,0:T(4,128)S(1)}, f32[4,3,1152]{2,1,0:T(4,128)S(1)}, f32[4,3,128]{2,1,0:T(4,128)S(1)}, f32[4,3,1152]{2,1,0:T(4,128)...) while((s32[]{:T(128)}, f32[4,3,128]{2,1,0:T(4,128)S(1)}, ...), condition=%wide.region_13.16_spmd, body=%wide.region_3.15_spmd.sunk | while | flops 6232500 | bytes 724117 | solution.py:208
  65.8 0.9 fusion.211
  67.4 0.9 fusion.211
  69.0 0.9 fusion.211
  70.6 0.9 fusion.211
  71.7 1.3 collective-permute-start.7
  73.0 4.5 %collective-permute-start.6 = (f32[3,1,1,640]{3,0,2,1:T(4,128)S(1)}, f32[3,1,1,640]{3,0,2,1:T(4,128)S(1)}, u32[]{:S(2)}, u32[]{:S(2)}) collective-permute-start(f32[3,1,1,640]{3,0,2,1:T(4,128)S(1)} %maximum_bitcast_fusion.2), channel_id=1, source_target_pairs={{0,4},{4,8},{8,12},{12,16},{16,20},{20,24},{24,28},{1,5},{5,9},{9,... | collective-permute-start | bytes 23048 | tf_op jit(solution)/shard_map/ppermute | solution.py:18
  77.5 0.7 pad_maximum_fusion.5
  78.2 1.1 collective-permute-done.8
  79.4 0.7 fusion.194
  80.1 1.5 collective-permute-start.9
  81.6 2.0 %collective-permute-done.9 = f32[7]{0:T(128)S(1)} collective-permute-done((f32[7]{0:T(128)S(1)}, f32[7]{0:T(128)S(1)}, u32[]{:S(2)}, u32[]{:S(2)}) %collective-permute-start.9) | collective-permute-done | bytes 60 | tf_op jit(solution)/shard_map/ppermute | solution.py:185
  83.7 17.1 %all-reduce.3 = f32[56]{0:T(128)S(1)} all-reduce(f32[56]{0:T(128)S(1)} %add_dynamic-update-slice_fusion.1), channel_id=3, replica_groups=mesh['cell'=8,'grp'=4] {'cell'}, use_global_device_ids=true, to_apply=%add.3 | all-reduce | flops 56 | bytes 448
  101.3 5.4 %all_gather.24 = f32[3,3,4,640]{3,0,2,1:T(4,128)S(1)} all-gather(f32[3,3,1,640]{3,0,2,1:T(4,128)S(1)} %pad_maximum_fusion.2), channel_id=1, replica_groups=mesh['cell'=8,'grp'=4] {'grp'}, dimensions={2}, use_global_device_ids=true | all-gather | bytes 115200 | tf_op jit(solution)/shard_map/all_gather | solution.py:119
  108.8 6.3 %while.80 = (s32[]{:T(128)}, f32[4,3,128]{2,1,0:T(4,128)S(1)}, f32[4,3,1152]{2,1,0:T(4,128)S(1)}, f32[4,3,128]{2,1,0:T(4,128)S(1)}, f32[4,3,1152]{2,1,0:T(4,128)...) while((s32[]{:T(128)}, f32[4,3,128]{2,1,0:T(4,128)S(1)}, ...), condition=%wide.region_31.35_spmd, body=%wide.region_21.34_spmd.sunk | while | flops 6232500 | bytes 724117 | solution.py:208
  109.5 0.9 fusion.216
  111.1 0.9 fusion.216
  112.7 0.9 fusion.216
  114.3 0.9 fusion.216
  115.3 2.4 %while.81 = (s32[]{:T(128)}, f32[3,128]{1,0:T(4,128)S(1)}, f32[3,3,1024]{2,0,1:T(4,128)S(1)}, f32[3,3,128]{2,1,0:T(4,128)S(1)}, f32[3,3,1024]{2,1,0:T(4,128)S(1)...) while((s32[]{:T(128)}, f32[3,128]{1,0:T(4,128)S(1)}, ...), condition=%wide.region_35.39_spmd, body=%wide.region_32.38_spmd.sunk | while | flops 2375092 | bytes 91217 | solution.py:212
  118.6 1.3 collective-permute-start.11
  119.9 4.5 %collective-permute-start.10 = (f32[3,1,1,640]{3,0,2,1:T(4,128)S(1)}, f32[3,1,1,640]{3,0,2,1:T(4,128)S(1)}, u32[]{:S(2)}, u32[]{:S(2)}) collective-permute-start(f32[3,1,1,640]{3,0,2,1:T(4,128)S(1)} %maximum_bitcast_fusion.3), channel_id=1, source_target_pairs={{0,4},{4,8},{8,12},{12,16},{16,20},{20,24},{24,28},{1,5},{5,9},{9,... | collective-permute-start | bytes 23048 | tf_op jit(solution)/shard_map/ppermute | solution.py:18
  124.4 0.7 pad_maximum_fusion.6
  125.2 1.1 collective-permute-done.12
  126.3 0.7 fusion.193
  127.0 1.5 collective-permute-start.13
  128.6 2.0 %collective-permute-done.13 = f32[7]{0:T(128)S(1)} collective-permute-done((f32[7]{0:T(128)S(1)}, f32[7]{0:T(128)S(1)}, u32[]{:S(2)}, u32[]{:S(2)}) %collective-permute-start.13) | collective-permute-done | bytes 60 | tf_op jit(solution)/shard_map/ppermute | solution.py:185
  130.7 20.0 %all-reduce.4 = f32[56]{0:T(128)S(1)} all-reduce(f32[56]{0:T(128)S(1)} %add_dynamic-update-slice_fusion), channel_id=4, replica_groups=mesh['cell'=8,'grp'=4] {'cell'}, use_global_device_ids=true, to_apply=%add.4 | all-reduce | flops 56 | bytes 448
  151.2 5.4 %all_gather.26 = f32[3,3,4,640]{3,0,2,1:T(4,128)S(1)} all-gather(f32[3,3,1,640]{3,0,2,1:T(4,128)S(1)} %pad_maximum_fusion.3), channel_id=1, replica_groups=mesh['cell'=8,'grp'=4] {'grp'}, dimensions={2}, use_global_device_ids=true | all-gather | bytes 115200 | tf_op jit(solution)/shard_map/all_gather | solution.py:119
  158.7 6.3 %while.82 = (s32[]{:T(128)}, f32[4,3,128]{2,1,0:T(4,128)S(1)}, f32[4,3,1152]{2,1,0:T(4,128)S(1)}, f32[4,3,128]{2,1,0:T(4,128)S(1)}, f32[4,3,1152]{2,1,0:T(4,128)...) while((s32[]{:T(128)}, f32[4,3,128]{2,1,0:T(4,128)S(1)}, ...), condition=%wide.region_49.53_spmd, body=%wide.region_39.52_spmd.sunk | while | flops 6232500 | bytes 724117 | solution.py:208
  159.4 0.9 fusion.221
  161.0 0.9 fusion.221
  162.5 0.9 fusion.221
  164.1 0.9 fusion.221
  165.7 2.4 %while.83 = (s32[]{:T(128)}, f32[3,128]{1,0:T(4,128)S(1)}, f32[3,3,1024]{2,0,1:T(4,128)S(1)}, f32[3,3,128]{2,1,0:T(4,128)S(1)}, f32[3,3,1024]{2,1,0:T(4,128)S(1)...) while((s32[]{:T(128)}, f32[3,128]{1,0:T(4,128)S(1)}, ...), condition=%wide.region_53.57_spmd, body=%wide.region_50.56_spmd.sunk | while | flops 2375092 | bytes 91217 | solution.py:212
  (394 shorter events, 32.4 us)
Async XLA Ops:
  0.6 7.5 %copy-start = (f32[3,384]{1,0:T(4,128)S(1)}, f32[3,384]{1,0:T(4,128)}, u32[]{:S(2)}) copy-start(f32[3,384]{1,0:T(4,128)} %param.29) | copy-start | bytes 13828
  0.6 7.5 %copy-start.1 = (f32[3,512]{1,0:T(4,128)S(1)}, f32[3,512]{1,0:T(4,128)}, u32[]{:S(2)}) copy-start(f32[3,512]{1,0:T(4,128)} %param.28) | copy-start | bytes 18436
  1.4 45.3 %collective-permute-start.1 = (f32[3,1,1,640]{3,0,2,1:T(4,128)S(1)}, f32[3,1,1,640]{3,0,2,1:T(4,128)S(1)}, u32[]{:S(2)}, u32[]{:S(2)}) collective-permute-start(f32[3,1,1,640]{3,0,2,1:T(4,128)S(1)} %maximum_bitcast_fusion.1), channel_id=1, source_target_pairs={{4,0},{8,4},{12,8},{16,12},{20,16},{24,20},{28,24},{5,1},{9,5},{13... | collective-permute-start | bytes 23048 | tf_op jit(solution)/shard_map/ppermute | solution.py:19
  2.7 44.0 %collective-permute-start = (f32[3,1,1,640]{3,0,2,1:T(4,128)S(1)}, f32[3,1,1,640]{3,0,2,1:T(4,128)S(1)}, u32[]{:S(2)}, u32[]{:S(2)}) collective-permute-start(f32[3,1,1,640]{3,0,2,1:T(4,128)S(1)} %maximum_bitcast_fusion.1), channel_id=1, source_target_pairs={{0,4},{4,8},{8,12},{12,16},{16,20},{20,24},{24,28},{1,5},{5,9},{9,... | collective-permute-start | bytes 23048 | tf_op jit(solution)/shard_map/ppermute | solution.py:18
  8.2 45.8 %collective-permute-start.3 = (f32[3,1,1,896]{3,0,2,1:T(4,128)S(1)}, f32[3,1,1,896]{3,0,2,1:T(4,128)S(1)}, u32[]{:S(2)}, u32[]{:S(2)}) collective-permute-start(f32[3,1,1,896]{3,0,2,1:T(4,128)S(1)} %maximum_bitcast_fusion), channel_id=1, source_target_pairs={{4,0},{8,4},{12,8},{16,12},{20,16},{24,20},{28,24},{5,1},{9,5},{13... | collective-permute-start | bytes 32264 | tf_op jit(solution)/shard_map/ppermute | solution.py:19
  9.5 44.5 %collective-permute-start.2 = (f32[3,1,1,896]{3,0,2,1:T(4,128)S(1)}, f32[3,1,1,896]{3,0,2,1:T(4,128)S(1)}, u32[]{:S(2)}, u32[]{:S(2)}) collective-permute-start(f32[3,1,1,896]{3,0,2,1:T(4,128)S(1)} %maximum_bitcast_fusion), channel_id=1, source_target_pairs={{0,4},{4,8},{8,12},{12,16},{16,20},{20,24},{24,28},{1,5},{5,9},{9,... | collective-permute-start | bytes 32264 | tf_op jit(solution)/shard_map/ppermute | solution.py:18
  15.0 0.7 copy-start.2
  15.0 1.3 copy-start.4
  17.3 4.3 %collective-permute-start.4 = (f32[7]{0:T(128)S(1)}, f32[7]{0:T(128)S(1)}, u32[]{:S(2)}, u32[]{:S(2)}) collective-permute-start(f32[7]{0:T(128)S(1)} %pad_maximum_fusion.4), channel_id=1, source_target_pairs={{0,1},{1,0},{2,3},{3,2},{4,5},{5,4},{6,7},{7,6},{8,9},{9,8},{10,11... | collective-permute-start | bytes 92 | tf_op jit(solution)/shard_map/ppermute | solution.py:185
  17.3 0.7 copy-start.7
  18.0 0.7 copy-start.8
  18.7 0.7 copy-start.9
  19.8 0.7 copy-start.10
  22.3 3.6 %collective-permute-start.5 = (f32[7]{0:T(128)S(1)}, f32[7]{0:T(128)S(1)}, u32[]{:S(2)}, u32[]{:S(2)}) collective-permute-start(f32[7]{0:T(128)S(1)} %fusion.195), channel_id=1, source_target_pairs={{0,2},{1,3},{2,0},{3,1},{4,6},{5,7},{6,4},{7,5},{8,10},{9,11},{10,... | collective-permute-start | bytes 92 | tf_op jit(solution)/shard_map/ppermute | solution.py:185
  61.7 2.4 %copy-start.5 = (f32[384]{0:T(512)S(1)}, f32[384]{0:T(512)}, u32[]{:S(2)}) copy-start(f32[384]{0:T(512)} %param.34) | copy-start | bytes 4612
  65.1 6.4 %copy-start.3 = (f32[3,512]{1,0:T(4,128)S(1)}, f32[3,512]{1,0:T(4,128)}, u32[]{:S(2)}) copy-start(f32[3,512]{1,0:T(4,128)} %param.31) | copy-start | bytes 18436
  65.2 6.4 %copy-start.6 = (f32[512]{0:T(512)S(1)}, f32[512]{0:T(512)}, u32[]{:S(2)}) copy-start(f32[512]{0:T(512)} %param.32) | copy-start | bytes 6148
  71.7 29.7 %collective-permute-start.7 = (f32[3,1,1,640]{3,0,2,1:T(4,128)S(1)}, f32[3,1,1,640]{3,0,2,1:T(4,128)S(1)}, u32[]{:S(2)}, u32[]{:S(2)}) collective-permute-start(f32[3,1,1,640]{3,0,2,1:T(4,128)S(1)} %maximum_bitcast_fusion.2), channel_id=1, source_target_pairs={{4,0},{8,4},{12,8},{16,12},{20,16},{24,20},{28,24},{5,1},{9,5},{13... | collective-permute-start | bytes 23048 | tf_op jit(solution)/shard_map/ppermute | solution.py:19
  73.0 28.4 %collective-permute-start.6 = (f32[3,1,1,640]{3,0,2,1:T(4,128)S(1)}, f32[3,1,1,640]{3,0,2,1:T(4,128)S(1)}, u32[]{:S(2)}, u32[]{:S(2)}) collective-permute-start(f32[3,1,1,640]{3,0,2,1:T(4,128)S(1)} %maximum_bitcast_fusion.2), channel_id=1, source_target_pairs={{0,4},{4,8},{8,12},{12,16},{16,20},{20,24},{24,28},{1,5},{5,9},{9,... | collective-permute-start | bytes 23048 | tf_op jit(solution)/shard_map/ppermute | solution.py:18
  78.2 1.2 collective-permute-start.8
  80.1 3.6 %collective-permute-start.9 = (f32[7]{0:T(128)S(1)}, f32[7]{0:T(128)S(1)}, u32[]{:S(2)}, u32[]{:S(2)}) collective-permute-start(f32[7]{0:T(128)S(1)} %fusion.194), channel_id=1, source_target_pairs={{0,2},{1,3},{2,0},{3,1},{4,6},{5,7},{6,4},{7,5},{8,10},{9,11},{10,... | collective-permute-start | bytes 92 | tf_op jit(solution)/shard_map/ppermute | solution.py:185
  118.6 32.6 %collective-permute-start.11 = (f32[3,1,1,640]{3,0,2,1:T(4,128)S(1)}, f32[3,1,1,640]{3,0,2,1:T(4,128)S(1)}, u32[]{:S(2)}, u32[]{:S(2)}) collective-permute-start(f32[3,1,1,640]{3,0,2,1:T(4,128)S(1)} %maximum_bitcast_fusion.3), channel_id=1, source_target_pairs={{4,0},{8,4},{12,8},{16,12},{20,16},{24,20},{28,24},{5,1},{9,5},{13... | collective-permute-start | bytes 23048 | tf_op jit(solution)/shard_map/ppermute | solution.py:19
  119.9 31.3 %collective-permute-start.10 = (f32[3,1,1,640]{3,0,2,1:T(4,128)S(1)}, f32[3,1,1,640]{3,0,2,1:T(4,128)S(1)}, u32[]{:S(2)}, u32[]{:S(2)}) collective-permute-start(f32[3,1,1,640]{3,0,2,1:T(4,128)S(1)} %maximum_bitcast_fusion.3), channel_id=1, source_target_pairs={{0,4},{4,8},{8,12},{12,16},{16,20},{20,24},{24,28},{1,5},{5,9},{9,... | collective-permute-start | bytes 23048 | tf_op jit(solution)/shard_map/ppermute | solution.py:18
  125.1 1.2 collective-permute-start.12
  127.0 3.6 %collective-permute-start.13 = (f32[7]{0:T(128)S(1)}, f32[7]{0:T(128)S(1)}, u32[]{:S(2)}, u32[]{:S(2)}) collective-permute-start(f32[7]{0:T(128)S(1)} %fusion.193), channel_id=1, source_target_pairs={{0,2},{1,3},{2,0},{3,1},{4,6},{5,7},{6,4},{7,5},{8,10},{9,11},{10,... | collective-permute-start | bytes 92 | tf_op jit(solution)/shard_map/ppermute | solution.py:185
